TPU v7x, 32 devices: a whole 2x2x4 slice. The times are simulated.
32 devices in a mesh: fft: 16 (over z, x, core), scal: 2 (over y).
Axes of the slice: x: 2, y: 2, z: 4, core: 2. Of those that a mesh axis runs over, the one named last changes fastest.
Arguments:
- scalar_state: float32 [2, 2, 256, 256, 128], P('scal', None, 'fft'), may hold values from -12 to 12
- velocity: bfloat16 [3, 256, 256, 256], P(None, 'fft', 'scal'), may hold values from -6 to 6
- species: int32 [2], P('scal'), may hold values from 0 to 63
- kappa_table: float32 [64], replicated, may hold values from 0.1 to 1
- dealias_bound: int32 [2], P('scal'), may hold values from 64 to 85
Outputs:
- new_state: float32 [2, 2, 256, 256, 128], P('scal', None, 'fft')
- kappa: float32 [2], P('scal')
All inputs are finite; a program needn't handle non-finite values.
Results may differ from a plain program's by a relative error of at most 0.0027.
Values may be sent and summed in bfloat16 or wider, within the bound.
A program may use at most 128 MiB of HBM per device.

v0:
```python
import math
import jax
import jax.numpy as jnp
from jax import lax
from jax.sharding import PartitionSpec as P

cfl_number = 0.2


def twiddle(size_in, size_out, length):
    row_index = jnp.arange(size_in, dtype=jnp.int32)[:, None]
    col_index = jnp.arange(size_out, dtype=jnp.int32)[None, :]
    angles = (row_index * col_index % length).astype(jnp.float32) * (2.0 * math.pi / length)
    norming = 1.0 / math.sqrt(length)
    return (jnp.cos(angles) * norming, jnp.sin(angles) * norming)


def build_tables(length):
    half_len = length // 2
    full_cos, full_sin = twiddle(length, length, length)
    inv_cos, inv_sin = twiddle(half_len, length, length)
    weight = jnp.where(jnp.arange(half_len, dtype=jnp.int32) == 0, 1.0, 2.0).astype(jnp.float32)[
        :, None
    ]
    fwd_cos, fwd_sin = twiddle(length, half_len, length)
    listed = (full_cos, full_sin, inv_cos * weight, inv_sin * weight, fwd_cos, fwd_sin)
    return tuple((matrix.astype(jnp.bfloat16) for matrix in listed))


def product(formula, operand, matrix):
    return jnp.einsum(formula, operand, matrix, preferred_element_type=jnp.float32)


def complex_section(real_part, imag_part, cos_matrix, sin_matrix, formula, inverse):
    real_cos = product(formula, real_part, cos_matrix)
    real_sin = product(formula, real_part, sin_matrix)
    imag_cos = product(formula, imag_part, cos_matrix)
    imag_sin = product(formula, imag_part, sin_matrix)
    if inverse:
        return (real_cos - imag_sin, real_sin + imag_cos)
    return (real_cos + imag_sin, imag_cos - real_sin)


def times_wave(wavenumber, real_part, imag_part):
    new_real = (-wavenumber * imag_part.astype(jnp.float32)).astype(jnp.bfloat16)
    new_imag = (wavenumber * real_part.astype(jnp.float32)).astype(jnp.bfloat16)
    return (new_real, new_imag)


def body(scalar_state, velocity, species, kappa_table, dealias_bound):
    ky_local = scalar_state.shape[2]
    length = scalar_state.shape[3]
    half_len = length // 2
    total_count = kappa_table.shape[0]
    full_cos, full_sin, inv_cos, inv_sin, fwd_cos, fwd_sin = build_tables(length)
    ky_index = lax.axis_index("fft") * ky_local + jnp.arange(ky_local, dtype=jnp.int32)
    ky_wave = jnp.where(ky_index < half_len, ky_index, ky_index - length).astype(jnp.float32)[
        :, None, None
    ]
    kz_index = jnp.arange(length, dtype=jnp.int32)
    signed_full = jnp.where(kz_index < half_len, kz_index, kz_index - length).astype(jnp.float32)
    kz_wave = signed_full[None, :, None]
    ky_whole = signed_full[:, None, None]
    kx_wave = jnp.arange(half_len, dtype=jnp.int32).astype(jnp.float32)[None, None, :]
    ksquare = kx_wave * kx_wave + ky_wave * ky_wave + kz_wave * kz_wave
    weight = jnp.where(kx_wave == 0.0, 1.0, 2.0).astype(jnp.float32)
    cell_count = float(length) ** 3
    step_size = cfl_number * 2.0 * math.pi / length
    speeds = lax.all_gather(velocity, "scal", axis=2, tiled=True)

    def finish_inverse(halves):
        y_section = complex_section(
            halves[0], halves[1], full_cos, full_sin, "...yzx,yw->...zwx", True
        )
        y_real = y_section[0].astype(jnp.bfloat16)
        y_imag = y_section[1].astype(jnp.bfloat16)
        return product("...zwk,kx->...zwx", y_real, inv_cos) - product(
            "...zwk,kx->...zwx", y_imag, inv_sin
        )

    def gradient_set(real_part, imag_part):
        pair_real = jnp.stack([real_part, -kz_wave * imag_part]).astype(jnp.bfloat16)
        pair_imag = jnp.stack([imag_part, kz_wave * real_part]).astype(jnp.bfloat16)
        z_section = complex_section(
            pair_real, pair_imag, full_cos, full_sin, "...ykx,kz->...yzx", True
        )
        z_real = z_section[0].astype(jnp.bfloat16)
        z_imag = z_section[1].astype(jnp.bfloat16)
        came_real, came_imag = (
            lax.all_to_all(z_real, "fft", split_axis=2, concat_axis=1, tiled=True),
            lax.all_to_all(z_imag, "fft", split_axis=2, concat_axis=1, tiled=True),
        )
        x_real, x_imag = times_wave(kx_wave, came_real[0], came_imag[0])
        y_real, y_imag = times_wave(ky_whole, came_real[0], came_imag[0])
        all_real = jnp.stack([x_real, y_real, came_real[1]])
        all_imag = jnp.stack([x_imag, y_imag, came_imag[1]])
        return finish_inverse((all_real, all_imag))

    def advect(gradients):
        total = speeds[0].astype(jnp.float32) * gradients[0]
        total = total + speeds[1].astype(jnp.float32) * gradients[1]
        total = total + speeds[2].astype(jnp.float32) * gradients[2]
        return total.astype(jnp.bfloat16)

    def finish_forward(halves):
        return complex_section(halves[0], halves[1], full_cos, full_sin, "...wzk,zv->...wvk", False)

    def tendency(advected, bound):
        real_x = product("zyx,xk->zyk", advected, fwd_cos).astype(jnp.bfloat16)
        imag_x = (-product("zyx,xk->zyk", advected, fwd_sin)).astype(jnp.bfloat16)
        y_section = complex_section(real_x, imag_x, full_cos, full_sin, "zyk,yw->wzk", False)
        y_real = y_section[0].astype(jnp.bfloat16)
        y_imag = y_section[1].astype(jnp.bfloat16)
        spectral = finish_forward(
            (
                lax.all_to_all(y_real, "fft", split_axis=0, concat_axis=1, tiled=True),
                lax.all_to_all(y_imag, "fft", split_axis=0, concat_axis=1, tiled=True),
            )
        )
        dealias_mask = (ksquare <= bound * bound).astype(jnp.float32)
        return (-dealias_mask * spectral[0], -dealias_mask * spectral[1])

    scalar = 0
    start_real = scalar_state[scalar, 0]
    start_imag = scalar_state[scalar, 1]
    energy = start_real * start_real + start_imag * start_imag
    local_var = [jnp.sum(weight * energy) / cell_count]
    local_grad = [jnp.sum(weight * ksquare * energy) / cell_count]
    gradients = gradient_set(start_real, start_imag)
    magnitude = jnp.sqrt(
        gradients[0] * gradients[0] + gradients[1] * gradients[1] + gradients[2] * gradients[2]
    )
    local_peak = [jnp.max(magnitude)]
    advect_saved = [advect(gradients)]
    var_part = jnp.stack(local_var)
    grad_part = jnp.stack(local_grad)
    peak_part = jnp.stack(local_peak)
    variance, mean_grad = lax.psum((var_part, grad_part), "fft")
    peak_value = lax.pmax(peak_part, "fft")
    matches = species[:, None] == jnp.arange(total_count, dtype=jnp.int32)[None, :]
    base_kappa = jnp.sum(jnp.where(matches, kappa_table[None, :], 0.0), axis=1)
    kappa = base_kappa * peak_value * jnp.sqrt(variance) / (mean_grad + 1e-06)
    scalar = 0
    start_real = scalar_state[scalar, 0]
    start_imag = scalar_state[scalar, 1]
    factor = jnp.exp(-kappa[scalar] * ksquare * step_size)
    bound = dealias_bound[scalar].astype(jnp.float32)
    first_real, first_imag = tendency(advect_saved[scalar], bound)
    mid_real = factor * (start_real + step_size * first_real)
    mid_imag = factor * (start_imag + step_size * first_imag)
    second_real, second_imag = tendency(advect(gradient_set(mid_real, mid_imag)), bound)
    new_real = factor * start_real + 0.5 * step_size * (factor * first_real + second_real)
    new_imag = factor * start_imag + 0.5 * step_size * (factor * first_imag + second_imag)
    updated_list = [jnp.stack([new_real, new_imag])]
    return (jnp.stack(updated_list), kappa)


def solution(mesh):
    placed = (
        P("scal", None, "fft", None, None),
        P(None, "fft", "scal", None),
        P("scal"),
        P(),
        P("scal"),
    )
    return jax.shard_map(
        body,
        mesh=mesh,
        in_specs=placed,
        out_specs=(P("scal", None, "fft", None, None), P("scal")),
        check_vma=False,
    )
```

profile of v0, /device:TPU:9, one launch (start us, length us, event | category | flops | bytes accessed | tf_op | source)
XLA Modules:
  0.0 545.5 jit_solution(1776327295158472400)
XLA Ops:
  7.2 2.7 bitcast_convert_fusion
  11.2 1.6 fusion.53
  12.8 1.6 fusion.48
  14.5 2.7 copy.48
  17.1 6.5 %all-to-all-start.1 = ((bf16[2,16,256,128]{3,1,0,2:T(8,128)(2,1)}), bf16[2,16,256,128]{3,1,0,2:T(8,128)(2,1)}, u32[]{:S(2)}, u32[]{:S(2)}) async-start(bf16[2,16,256,128]{3,1,0,2:T(8,128)(2,1)} %copy.48), calls=%async_computation.1 | async-start | bytes 4194304 | tf_op jit(solution)/shard_map/all_to_all | solution.py:90
  23.7 1.6 fusion.54
  25.3 1.6 fusion.47
  26.9 2.7 copy.43
  29.6 40.2 %all-to-all-done.1 = bf16[2,16,256,128]{3,1,0,2:T(8,128)(2,1)} async-done(((bf16[2,16,256,128]{3,1,0,2:T(8,128)(2,1)}), bf16[2,16,256,128]{3,1,0,2:T(8,128)(2,1)}, u32[]{:S(2)}, u32[]{:S(2)}) %all-to-all-start.1) | async-done | bytes 2097184 | tf_op jit(solution)/shard_map/all_to_all | solution.py:90
  69.9 6.1 %all-to-all-start = ((bf16[2,16,256,128]{3,1,0,2:T(8,128)(2,1)}), bf16[2,16,256,128]{3,1,0,2:T(8,128)(2,1)S(1)}, u32[]{:S(2)}, u32[]{:S(2)}) async-start(bf16[2,16,256,128]{3,1,0,2:T(8,128)(2,1)} %copy.43), calls=%async_computation | async-start | bytes 4194304 | tf_op jit(solution)/shard_map/all_to_all | solution.py:91
  76.7 2.4 copy.49
  79.1 1.7 slice_convert_fusion.2
  82.3 39.8 %all-to-all-done = bf16[2,16,256,128]{3,1,0,2:T(8,128)(2,1)S(1)} async-done(((bf16[2,16,256,128]{3,1,0,2:T(8,128)(2,1)}), bf16[2,16,256,128]{3,1,0,2:T(8,128)(2,1)S(1)}, u32[]{:S(2)}, u32[]{:S(2)}) %all-to-all-start) | async-done | bytes 2097184 | tf_op jit(solution)/shard_map/all_to_all | solution.py:91
  126.5 4.6 fusion.58
  131.1 4.5 fusion.57
  136.5 11.1 %fusion.7 = f32[3,16,256,256]{3,2,1,0:T(8,128)} fusion(f32[256,3,16,128]{3,0,2,1:T(8,128)} %fusion.58, bf16[1,256,16,128]{3,1,2,0:T(8,128)(2,1)S(1)} %copy.56, bf16[1,256,16,128]{3,1,2,0:T(8,128)(2,1)S(1)} %get-tuple-element.27, bf16[1,256,16,128]{3,1,2,0:T(8,128)(2,1)S(1)} %get-tuple-element.26, f32[128]{0:T(128)S(1)} %fusion.137), kind=kOutput, calls=%fused_computation.28 | convolution fusion | flops 1624768512 | bytes 22020608 | tf_op jit(solution)/shard_map/...zwk,kx->...zwx/dot_general | solution.py:31
  147.5 11.4 %convolution_subtract_fusion.1 = f32[3,16,256,256]{3,2,1,0:T(8,128)} fusion(f32[3,16,256,256]{3,2,1,0:T(8,128)} %fusion.7, f32[256,3,16,128]{3,0,2,1:T(8,128)} %fusion.57, bf16[1,256,16,128]{3,1,2,0:T(8,128)(2,1)S(1)} %copy.56, bf16[1,256,16,128]{3,1,2,0:T(8,128)(2,1)S(1)} %get-tuple-element.27, bf16[1,256,16,128]{3,1,2,0:T(8,128)(2,1)S(1)} %get-tuple-element.26, ...), kind=kOutput, calls=%fused_computation.11 | convolution fusion | flops 1627914240 | bytes 34603520 | tf_op jit(solution)/shard_map/...zwk,kx->...zwx/dot_general | solution.py:31
  159.2 8.5 %sqrt_reduce_fusion = (f32[]{:T(128)}, bf16[16,256,256]{2,1,0:T(8,128)(2,1)S(1)}) fusion(f32[3,16,256,256]{3,2,1,0:T(8,128)} %convolution_subtract_fusion.1, bf16[3,16,256,256]{3,2,1,0:T(8,128)(2,1)} %all-gather.2.cloned.1.call-done), kind=kLoop, calls=%fused_computation.19 | loop fusion | flops 15728639 | bytes 20971524 | tf_op jit(solution)/shard_map/reduce_max | solution.py:133
  171.3 1.4 subtract_convert_fusion.5
  172.7 1.6 copy.59
  174.3 6.5 %all-to-all-start.3 = ((bf16[256,16,128]{2,1,0:T(8,128)(2,1)}), bf16[256,16,128]{2,1,0:T(8,128)(2,1)S(1)}, u32[]{:S(2)}, u32[]{:S(2)}) async-start(bf16[256,16,128]{2,1,0:T(8,128)(2,1)} %copy.59), calls=%async_computation.3 | async-start | bytes 2097152 | tf_op jit(solution)/shard_map/all_to_all | solution.py:117
  182.2 1.4 add_convert_fusion.5
  183.5 1.6 copy.57
  185.2 20.6 %all-to-all-done.3 = bf16[256,16,128]{2,1,0:T(8,128)(2,1)S(1)} async-done(((bf16[256,16,128]{2,1,0:T(8,128)(2,1)}), bf16[256,16,128]{2,1,0:T(8,128)(2,1)S(1)}, u32[]{:S(2)}, u32[]{:S(2)}) %all-to-all-start.3) | async-done | bytes 1048608 | tf_op jit(solution)/shard_map/all_to_all | solution.py:117
  205.8 4.8 all-to-all-start.2
  210.6 3.5 fusion.25
  215.5 35.4 %all-reduce = (f32[1]{0:T(128)}, f32[1]{0:T(128)}) all-reduce(f32[1]{0:T(128)} %bitcast.31, f32[1]{0:T(128)} %bitcast.32), channel_id=1, replica_groups=mesh['fft'=16,'scal'=2] {'fft'}, use_global_device_ids=true, to_apply=%region_4.5 | all-reduce | flops 2 | bytes 16 | tf_op jit(solution)/shard_map/psum | solution.py:138
  254.2 27.1 %pmax.7 = f32[1]{0:T(128)} all-reduce(f32[1]{0:T(128)} %bitcast.28), channel_id=1, replica_groups=mesh['fft'=16,'scal'=2] {'fft'}, use_global_device_ids=true, to_apply=%region_2.3 | all-reduce | flops 1 | bytes 8 | tf_op jit(solution)/shard_map/pmax | solution.py:139
  284.2 1.5 copy.58
  287.0 1.5 bitcast_multiply_fusion.2
  288.5 1.5 bitcast_multiply_fusion.3
  290.0 1.4 copy-done.1
  292.9 1.6 fusion.51
  294.5 1.6 fusion.50
  296.1 2.7 copy.66
  298.8 13.1 %all-to-all-start.5 = ((bf16[2,16,256,128]{3,1,0,2:T(8,128)(2,1)}), bf16[2,16,256,128]{3,1,0,2:T(8,128)(2,1)}, u32[]{:S(2)}, u32[]{:S(2)}) async-start(bf16[2,16,256,128]{3,1,0,2:T(8,128)(2,1)} %copy.66), calls=%async_computation.5 | async-start | bytes 4194304 | tf_op jit(solution)/shard_map/all_to_all | solution.py:90
  311.9 3.0 fusion.52
  314.9 1.6 fusion.49
  316.5 2.7 copy.61
  319.3 38.8 %all-to-all-done.5 = bf16[2,16,256,128]{3,1,0,2:T(8,128)(2,1)} async-done(((bf16[2,16,256,128]{3,1,0,2:T(8,128)(2,1)}), bf16[2,16,256,128]{3,1,0,2:T(8,128)(2,1)}, u32[]{:S(2)}, u32[]{:S(2)}) %all-to-all-start.5) | async-done | bytes 2097184 | tf_op jit(solution)/shard_map/all_to_all | solution.py:90
  358.1 6.1 %all-to-all-start.4 = ((bf16[2,16,256,128]{3,1,0,2:T(8,128)(2,1)}), bf16[2,16,256,128]{3,1,0,2:T(8,128)(2,1)}, u32[]{:S(2)}, u32[]{:S(2)}) async-start(bf16[2,16,256,128]{3,1,0,2:T(8,128)(2,1)} %copy.61), calls=%async_computation.4 | async-start | bytes 4194304 | tf_op jit(solution)/shard_map/all_to_all | solution.py:91
  364.2 2.4 copy.67
  366.6 1.7 slice_convert_fusion
  368.8 41.5 %all-to-all-done.4 = bf16[2,16,256,128]{3,1,0,2:T(8,128)(2,1)} async-done(((bf16[2,16,256,128]{3,1,0,2:T(8,128)(2,1)}), bf16[2,16,256,128]{3,1,0,2:T(8,128)(2,1)}, u32[]{:S(2)}, u32[]{:S(2)}) %all-to-all-start.4) | async-done | bytes 2097184 | tf_op jit(solution)/shard_map/all_to_all | solution.py:91
  410.4 2.4 copy.62
  414.3 4.6 fusion.56
  418.8 4.5 fusion.55
  425.3 1.8 multiply_convert_fusion.1
  427.2 11.9 %fusion.12 = f32[3,16,256,256]{3,2,1,0:T(8,128)} fusion(f32[256,3,16,128]{3,0,2,1:T(8,128)} %fusion.56, bf16[1,256,16,128]{3,1,2,0:T(8,128)(2,1)} %copy.74, bf16[1,256,16,128]{3,1,2,0:T(8,128)(2,1)} %get-tuple-element.19, bf16[1,256,16,128]{3,1,2,0:T(8,128)(2,1)S(1)} %get-tuple-element.18, f32[128]{0:T(128)S(1)} %fusion.137), kind=kOutput, calls=%fused_computation.31 | convolution fusion | flops 1624768512 | bytes 22020608 | tf_op jit(solution)/shard_map/...zwk,kx->...zwx/dot_general | solution.py:31
  439.1 12.0 %convolution_subtract_fusion = f32[3,16,256,256]{3,2,1,0:T(8,128)} fusion(f32[3,16,256,256]{3,2,1,0:T(8,128)} %fusion.12, f32[256,3,16,128]{3,0,2,1:T(8,128)} %fusion.55, bf16[1,256,16,128]{3,1,2,0:T(8,128)(2,1)} %copy.74, bf16[1,256,16,128]{3,1,2,0:T(8,128)(2,1)} %get-tuple-element.19, bf16[1,256,16,128]{3,1,2,0:T(8,128)(2,1)S(1)} %get-tuple-element.18, ...), kind=kOutput, calls=%fused_computation.10 | convolution fusion | flops 1627914240 | bytes 34603520 | tf_op jit(solution)/shard_map/...zwk,kx->...zwx/dot_general | solution.py:31
  451.1 7.2 %fusion.42 = bf16[16,256,256]{2,1,0:T(8,128)(2,1)S(1)} fusion(f32[3,16,256,256]{3,2,1,0:T(8,128)} %convolution_subtract_fusion, bf16[3,16,256,256]{3,2,1,0:T(8,128)(2,1)} %all-gather.2.cloned.1.call-done), kind=kLoop, calls=%fused_computation.59 | loop fusion | flops 9437184 | bytes 20971520 | tf_op jit(solution)/shard_map/add | solution.py:102
  462.1 1.4 subtract_convert_fusion.4
  463.5 1.6 copy.77
  465.1 6.4 %all-to-all-start.7 = ((bf16[256,16,128]{2,1,0:T(8,128)(2,1)}), bf16[256,16,128]{2,1,0:T(8,128)(2,1)}, u32[]{:S(2)}, u32[]{:S(2)}) async-start(bf16[256,16,128]{2,1,0:T(8,128)(2,1)} %copy.77), calls=%async_computation.7 | async-start | bytes 2097152 | tf_op jit(solution)/shard_map/all_to_all | solution.py:117
  474.2 1.7 copy.75
  475.9 20.5 %all-to-all-done.7 = bf16[256,16,128]{2,1,0:T(8,128)(2,1)} async-done(((bf16[256,16,128]{2,1,0:T(8,128)(2,1)}), bf16[256,16,128]{2,1,0:T(8,128)(2,1)}, u32[]{:S(2)}, u32[]{:S(2)}) %all-to-all-start.7) | async-done | bytes 1048608 | tf_op jit(solution)/shard_map/all_to_all | solution.py:117
  496.4 4.8 all-to-all-start.6
  501.1 1.5 copy.78
  502.6 2.7 fusion.81
  505.3 20.8 %all-to-all-done.6 = bf16[256,16,128]{2,1,0:T(8,128)(2,1)} async-done(((bf16[256,16,128]{2,1,0:T(8,128)(2,1)}), bf16[256,16,128]{2,1,0:T(8,128)(2,1)}, u32[]{:S(2)}, u32[]{:S(2)}) %all-to-all-start.6) | async-done | bytes 1048608 | tf_op jit(solution)/shard_map/all_to_all | solution.py:116
  526.2 1.6 copy.76
  529.2 3.8 fusion.39
  532.9 2.1 fusion.35
  535.0 2.3 maximum_bitcast_fusion
  (80 shorter events, 30.7 us)
Async XLA Ops:
  7.2 3.5 copy-start
  11.2 1.6 copy-start.9
  17.1 52.7 %all-to-all-start.1 = ((bf16[2,16,256,128]{3,1,0,2:T(8,128)(2,1)}), bf16[2,16,256,128]{3,1,0,2:T(8,128)(2,1)}, u32[]{:S(2)}, u32[]{:S(2)}) async-start(bf16[2,16,256,128]{3,1,0,2:T(8,128)(2,1)} %copy.48), calls=%async_computation.1 | async-start | bytes 4194304 | tf_op jit(solution)/shard_map/all_to_all | solution.py:90
  23.7 1.6 copy-start.10
  69.9 52.3 %all-to-all-start = ((bf16[2,16,256,128]{3,1,0,2:T(8,128)(2,1)}), bf16[2,16,256,128]{3,1,0,2:T(8,128)(2,1)S(1)}, u32[]{:S(2)}, u32[]{:S(2)}) async-start(bf16[2,16,256,128]{3,1,0,2:T(8,128)(2,1)} %copy.43), calls=%async_computation | async-start | bytes 4194304 | tf_op jit(solution)/shard_map/all_to_all | solution.py:91
  76.0 83.2 %all-gather.2.cloned.1.call-start = ((), (), s32[]{:S(2)}) async-start(), calls=%async_computation.8 | async-start | bytes 9437184 | tf_op jit(solution)/shard_map/all_gather | solution.py:69
  123.5 1.6 copy-start.12
  125.3 1.2 copy-start.15
  174.3 31.4 %all-to-all-start.3 = ((bf16[256,16,128]{2,1,0:T(8,128)(2,1)}), bf16[256,16,128]{2,1,0:T(8,128)(2,1)S(1)}, u32[]{:S(2)}, u32[]{:S(2)}) async-start(bf16[256,16,128]{2,1,0:T(8,128)(2,1)} %copy.59), calls=%async_computation.3 | async-start | bytes 2097152 | tf_op jit(solution)/shard_map/all_to_all | solution.py:117
  205.8 78.4 %all-to-all-start.2 = ((bf16[256,16,128]{2,1,0:T(8,128)(2,1)}), bf16[256,16,128]{2,1,0:T(8,128)(2,1)}, u32[]{:S(2)}, u32[]{:S(2)}) async-start(bf16[256,16,128]{2,1,0:T(8,128)(2,1)} %copy.57), calls=%async_computation.2 | async-start | bytes 2097152 | tf_op jit(solution)/shard_map/all_to_all | solution.py:116
  210.6 43.0 %copy-start.16 = (f32[64]{0:T(128)S(1)}, f32[64]{0:T(128)}, u32[]{:S(2)}) copy-start(f32[64]{0:T(128)} %param.8) | copy-start | bytes 772
  288.5 1.5 copy-start.3
  288.5 2.9 copy-start.1
  292.8 1.6 copy-start.4
  292.8 1.6 copy-start.5
  292.9 1.7 copy-start.7
  298.8 59.3 %all-to-all-start.5 = ((bf16[2,16,256,128]{3,1,0,2:T(8,128)(2,1)}), bf16[2,16,256,128]{3,1,0,2:T(8,128)(2,1)}, u32[]{:S(2)}, u32[]{:S(2)}) async-start(bf16[2,16,256,128]{3,1,0,2:T(8,128)(2,1)} %copy.66), calls=%async_computation.5 | async-start | bytes 4194304 | tf_op jit(solution)/shard_map/all_to_all | solution.py:90
  311.9 3.0 copy-start.6
  311.9 3.0 copy-start.8
  358.1 52.3 %all-to-all-start.4 = ((bf16[2,16,256,128]{3,1,0,2:T(8,128)(2,1)}), bf16[2,16,256,128]{3,1,0,2:T(8,128)(2,1)}, u32[]{:S(2)}, u32[]{:S(2)}) async-start(bf16[2,16,256,128]{3,1,0,2:T(8,128)(2,1)} %copy.61), calls=%async_computation.4 | async-start | bytes 4194304 | tf_op jit(solution)/shard_map/all_to_all | solution.py:91
  423.4 1.8 copy-start.11
  459.6 1.2 copy-start.13
  465.1 31.3 %all-to-all-start.7 = ((bf16[256,16,128]{2,1,0:T(8,128)(2,1)}), bf16[256,16,128]{2,1,0:T(8,128)(2,1)}, u32[]{:S(2)}, u32[]{:S(2)}) async-start(bf16[256,16,128]{2,1,0:T(8,128)(2,1)} %copy.77), calls=%async_computation.7 | async-start | bytes 2097152 | tf_op jit(solution)/shard_map/all_to_all | solution.py:117
  471.5 1.3 copy-start.14
  496.4 29.8 %all-to-all-start.6 = ((bf16[256,16,128]{2,1,0:T(8,128)(2,1)}), bf16[256,16,128]{2,1,0:T(8,128)(2,1)}, u32[]{:S(2)}, u32[]{:S(2)}) async-start(bf16[256,16,128]{2,1,0:T(8,128)(2,1)} %copy.75), calls=%async_computation.6 | async-start | bytes 2097152 | tf_op jit(solution)/shard_map/all_to_all | solution.py:116
  526.2 3.0 copy-start.2
Sparse Core Ops, SparseCore 0:
  78.3 80.8 all-gather.1
where the time goes:
time: 554 us; the launch traced here: 546 us
  waiting for transfers between devices  223 us (40%)
  matrix products  110 us (20%)
  blocking collectives  62.5 us (11%)
  starting transfers between devices  54.8 us (10%)
  local copies, waits for them, and re-layouts  41.8 us (8%)
  other arithmetic  32.5 us (6%)
  between operations  21.2 us (4%)
    dot_general x36, matrix products, product(): jnp.einsum(formula, operand, matrix, preferred_element_type=jnp.float32)  110 us
    all_to_all x2, waiting for transfers between devices, gradient_set(): lax.all_to_all(z_imag, 'fft', split_axis=2, concat_axis=1, tiled=True)  81.3 us
    all_to_all x2, waiting for transfers between devices, gradient_set(): lax.all_to_all(z_real, 'fft', split_axis=2, concat_axis=1, tiled=True)  79.1 us
    all_to_all x2, waiting for transfers between devices, tendency(): lax.all_to_all(y_imag, 'fft', split_axis=0, concat_axis=1, tiled=True)  41.1 us
    psum x1, blocking collectives, body(): variance, mean_grad = lax.psum((var_part, grad_part), 'fft')  35.4 us
    pmax x1, blocking collectives, body(): peak_value = lax.pmax(peak_part, 'fft')  27.1 us
    all_to_all x2, waiting for transfers between devices, tendency(): lax.all_to_all(y_real, 'fft', split_axis=0, concat_axis=1, tiled=True)  20.8 us
    all_to_all x2, starting transfers between devices, gradient_set(): lax.all_to_all(z_real, 'fft', split_axis=2, concat_axis=1, tiled=True)  19.6 us
  transfers between devices with their start and end apart: 9, of which 8 were waited for; matrix products, arithmetic and copies ran while one was open for 14% of the time, Pallas kernels for 0%

commit v1 on v0

--- a/solution.py
+++ b/solution.py
@@ -1,3 +1,4 @@
+import functools
 import math
 import jax
 import jax.numpy as jnp
@@ -5,6 +6,42 @@
 from jax.sharding import PartitionSpec as P
 
 cfl_number = 0.2
+
+
+def _mark_roots(page, on_dim, mine_x):
+    aux, plain = (page.shape[:on_dim], page.shape[on_dim + 1 :])
+    z_new = page.reshape(*aux, mine_x, -1, *plain)
+    return jnp.moveaxis(z_new, on_dim, 0)
+
+
+def carry_zone(incoming_x, array_axis):
+    incoming_x = jnp.moveaxis(incoming_x, 0, array_axis)
+    item_now = incoming_x.shape
+    return incoming_x.reshape(
+        *item_now[:array_axis],
+        item_now[array_axis] * item_now[array_axis + 1],
+        *item_now[array_axis + 2 :]
+    )
+
+
+def perform_sample_over_axis(state, which_axis, message, chunk):
+    all_values = lax.axis_size(which_axis)
+    vec_out = lax.axis_index(which_axis)
+    x_now, piece_next = (all_values, vec_out)
+    high = _mark_roots(state, chunk, x_now)
+    kept_arr = high
+    for idx in range(1, x_now):
+        state_now, block_out = ((piece_next + idx) % x_now, (piece_next - idx) % x_now)
+        small = lax.dynamic_index_in_dim(high, state_now, 0)
+        f_next = range(x_now)
+        side_arr = map(lambda num: (num, (num + idx) % x_now), f_next)
+        arr_out = list(side_arr)
+        extra = lax.ppermute(small, which_axis, arr_out)
+        kept_arr = lax.dynamic_update_slice_in_dim(kept_arr, extra, block_out, axis=0)
+    return carry_zone(kept_arr, message)
+
+
+obtain_indices = functools.partial(perform_sample_over_axis, which_axis="fft", message=1, chunk=0)
 
 
 def twiddle(size_in, size_out, length):
@@ -114,7 +151,7 @@
         spectral = finish_forward(
             (
                 lax.all_to_all(y_real, "fft", split_axis=0, concat_axis=1, tiled=True),
-                lax.all_to_all(y_imag, "fft", split_axis=0, concat_axis=1, tiled=True),
+                obtain_indices(y_imag),
             )
         )
         dealias_mask = (ksquare <= bound * bound).astype(jnp.float32)

time: 554 us -> 564 us (1.018)
  starting transfers between devices: 54.8 us -> 125 us
  waiting for transfers between devices: 223 us -> 167 us
    ppermute x0 -> x30, starting transfers between devices: none -> 86.4 us  [perform_sample_over_axis(): extra = lax.ppermute(small, which_axis, arr_out)]
    all_to_all x2 -> x0, waiting for transfers between devices: 41.1 us -> none  [tendency(): lax.all_to_all(y_imag, 'fft', split_axis=0, concat_axis=1, tiled=True)]
    all_to_all x2, waiting for transfers between devices: 20.8 us -> 0.01 us  [tendency(): lax.all_to_all(y_real, 'fft', split_axis=0, concat_axis=1, tiled=True)]
    all_to_all x2 -> x0, starting transfers between devices: 12.9 us -> none  [tendency(): lax.all_to_all(y_imag, 'fft', split_axis=0, concat_axis=1, tiled=True)]
    all_to_all x2, starting transfers between devices: 19.6 us -> 12.5 us  [gradient_set(): lax.all_to_all(z_real, 'fft', split_axis=2, concat_axis=1, tiled=True)]
    ppermute x0 -> x30, waiting for transfers between devices: none -> 6.09 us  [perform_sample_over_axis(): extra = lax.ppermute(small, which_axis, arr_out)]
  transfers between devices with their start and end apart: 9 -> 37, of which waited for: 8 -> 10; matrix products, arithmetic and copies ran while one was open for 14% -> 13% of each run, Pallas kernels for 0% -> 0%
where the time goes in v1:
time: 564 us; the launch traced here: 554 us
  waiting for transfers between devices  167 us (30%)
  starting transfers between devices  125 us (22%)
  matrix products  113 us (20%)
  blocking collectives  57.6 us (10%)
  local copies, waits for them, and re-layouts  39.7 us (7%)
  other arithmetic  30.7 us (5%)
  between operations  21.7 us (4%)
    dot_general x36, matrix products, product(): jnp.einsum(formula, operand, matrix, preferred_element_type=jnp.float32)  113 us
    ppermute x30, starting transfers between devices, perform_sample_over_axis(): extra = lax.ppermute(small, which_axis, arr_out)  86.4 us
    all_to_all x2, waiting for transfers between devices, gradient_set(): lax.all_to_all(z_imag, 'fft', split_axis=2, concat_axis=1, tiled=True)  81.1 us
    all_to_all x2, waiting for transfers between devices, gradient_set(): lax.all_to_all(z_real, 'fft', split_axis=2, concat_axis=1, tiled=True)  79 us
    psum x1, blocking collectives, body(): variance, mean_grad = lax.psum((var_part, grad_part), 'fft')  32.7 us
    pmax x1, blocking collectives, body(): peak_value = lax.pmax(peak_part, 'fft')  24.8 us
    all_to_all x2, starting transfers between devices, tendency(): lax.all_to_all(y_real, 'fft', split_axis=0, concat_axis=1, tiled=True)  12.9 us
    all_to_all x2, starting transfers between devices, gradient_set(): lax.all_to_all(z_real, 'fft', split_axis=2, concat_axis=1, tiled=True)  12.5 us
  transfers between devices with their start and end apart: 37, of which 10 were waited for; matrix products, arithmetic and copies ran while one was open for 13% of the time, Pallas kernels for 0%

profile of v1, /device:TPU:9, one launch (start us, length us, event | category | flops | bytes accessed | tf_op | source)
XLA Modules:
  0.0 554.0 jit_solution(6600580647465836914)
XLA Ops:
  7.2 2.7 bitcast_convert_fusion
  14.5 2.7 copy.46
  17.1 6.5 %all-to-all-start.1 = ((bf16[2,16,256,128]{3,1,0,2:T(8,128)(2,1)}), bf16[2,16,256,128]{3,1,0,2:T(8,128)(2,1)}, u32[]{:S(2)}, u32[]{:S(2)}) async-start(bf16[2,16,256,128]{3,1,0,2:T(8,128)(2,1)} %copy.46), calls=%async_computation.1 | async-start | bytes 4194304 | tf_op jit(solution)/shard_map/all_to_all | solution.py:127
  26.9 2.7 copy.41
  29.7 40.2 %all-to-all-done.1 = bf16[2,16,256,128]{3,1,0,2:T(8,128)(2,1)} async-done(((bf16[2,16,256,128]{3,1,0,2:T(8,128)(2,1)}), bf16[2,16,256,128]{3,1,0,2:T(8,128)(2,1)}, u32[]{:S(2)}, u32[]{:S(2)}) %all-to-all-start.1) | async-done | bytes 2097184 | tf_op jit(solution)/shard_map/all_to_all | solution.py:127
  69.9 6.1 %all-to-all-start = ((bf16[2,16,256,128]{3,1,0,2:T(8,128)(2,1)}), bf16[2,16,256,128]{3,1,0,2:T(8,128)(2,1)S(1)}, u32[]{:S(2)}, u32[]{:S(2)}) async-start(bf16[2,16,256,128]{3,1,0,2:T(8,128)(2,1)} %copy.41), calls=%async_computation | async-start | bytes 4194304 | tf_op jit(solution)/shard_map/all_to_all | solution.py:128
  76.9 2.4 copy.47
  79.3 1.7 slice_convert_fusion.2
  82.5 39.6 %all-to-all-done = bf16[2,16,256,128]{3,1,0,2:T(8,128)(2,1)S(1)} async-done(((bf16[2,16,256,128]{3,1,0,2:T(8,128)(2,1)}), bf16[2,16,256,128]{3,1,0,2:T(8,128)(2,1)S(1)}, u32[]{:S(2)}, u32[]{:S(2)}) %all-to-all-start) | async-done | bytes 2097184 | tf_op jit(solution)/shard_map/all_to_all | solution.py:128
  126.5 4.6 fusion.58
  131.1 4.6 fusion.57
  136.5 11.1 %fusion.7 = f32[3,16,256,256]{3,2,1,0:T(8,128)} fusion(f32[256,3,16,128]{3,0,2,1:T(8,128)} %fusion.58, bf16[1,256,16,128]{3,1,2,0:T(8,128)(2,1)S(1)} %copy.54, bf16[1,256,16,128]{3,1,2,0:T(8,128)(2,1)S(1)} %get-tuple-element.27, bf16[1,256,16,128]{3,1,2,0:T(8,128)(2,1)S(1)} %get-tuple-element.26, f32[128]{0:T(128)S(1)} %fusion.177), kind=kOutput, calls=%fused_computation.28 | convolution fusion | flops 1624768512 | bytes 22020608 | tf_op jit(solution)/shard_map/...zwk,kx->...zwx/dot_general | solution.py:68
  147.6 11.4 %convolution_subtract_fusion.1 = f32[3,16,256,256]{3,2,1,0:T(8,128)} fusion(f32[3,16,256,256]{3,2,1,0:T(8,128)} %fusion.7, f32[256,3,16,128]{3,0,2,1:T(8,128)} %fusion.57, bf16[1,256,16,128]{3,1,2,0:T(8,128)(2,1)S(1)} %copy.54, bf16[1,256,16,128]{3,1,2,0:T(8,128)(2,1)S(1)} %get-tuple-element.27, bf16[1,256,16,128]{3,1,2,0:T(8,128)(2,1)S(1)} %get-tuple-element.26, ...), kind=kOutput, calls=%fused_computation.11 | convolution fusion | flops 1627914240 | bytes 34603520 | tf_op jit(solution)/shard_map/...zwk,kx->...zwx/dot_general | solution.py:68
  159.2 8.5 %sqrt_reduce_fusion = (f32[]{:T(128)}, bf16[16,256,256]{2,1,0:T(8,128)(2,1)S(1)}) fusion(f32[3,16,256,256]{3,2,1,0:T(8,128)} %convolution_subtract_fusion.1, bf16[3,16,256,256]{3,2,1,0:T(8,128)(2,1)} %all-gather.2.cloned.1.call-done), kind=kLoop, calls=%fused_computation.19 | loop fusion | flops 15728639 | bytes 20971524 | tf_op jit(solution)/shard_map/reduce_max | solution.py:170
  171.3 2.7 fusion.91
  175.4 1.7 copy.55
  177.0 6.5 %all-to-all-start.2 = ((bf16[256,16,128]{2,1,0:T(8,128)(2,1)}), bf16[256,16,128]{2,1,0:T(8,128)(2,1)}, u32[]{:S(2)}, u32[]{:S(2)}) async-start(bf16[256,16,128]{2,1,0:T(8,128)(2,1)} %copy.55), calls=%async_computation.2 | async-start | bytes 2097152 | tf_op jit(solution)/shard_map/all_to_all | solution.py:153
  183.5 3.1 subtract_convert_fusion.5
  191.2 32.7 %all-reduce = (f32[1]{0:T(128)}, f32[1]{0:T(128)}) all-reduce(f32[1]{0:T(128)} %bitcast.31, f32[1]{0:T(128)} %bitcast.32), channel_id=1, replica_groups=mesh['fft'=16,'scal'=2] {'fft'}, use_global_device_ids=true, to_apply=%region_4.5 | all-reduce | flops 2 | bytes 16 | tf_op jit(solution)/shard_map/psum | solution.py:175
  226.9 2.9 collective-permute-start.1
  230.5 24.8 %pmax.7 = f32[1]{0:T(128)} all-reduce(f32[1]{0:T(128)} %bitcast.28), channel_id=1, replica_groups=mesh['fft'=16,'scal'=2] {'fft'}, use_global_device_ids=true, to_apply=%region_2.3 | all-reduce | flops 1 | bytes 8 | tf_op jit(solution)/shard_map/pmax | solution.py:176
  256.8 2.0 collective-permute-start.2
  258.8 3.2 collective-permute-start.3
  261.9 6.9 %collective-permute-start.4 = (bf16[1,16,16,128]{3,1,0,2:T(8,128)(2,1)S(1)}, bf16[1,16,16,128]{3,1,0,2:T(8,128)(2,1)S(1)}, u32[]{:S(2)}, u32[]{:S(2)}) collective-permute-start(bf16[1,16,16,128]{3,1,0,2:T(8,128)(2,1)S(1)} %get-tuple-element.59), channel_id=1, source_target_pairs={{0,10},{2,12},{4,14},{6,16},{8,18},{10,20},{12,22},{14,24},{16,26}... | collective-permute-start | bytes 196616 | tf_op jit(solution)/shard_map/ppermute | solution.py:39
  268.8 2.9 collective-permute-start.5
  272.0 2.6 collective-permute-start.7
  274.6 2.2 collective-permute-start.8
  276.8 2.0 collective-permute-start.9
  280.2 3.3 collective-permute-start.11
  283.5 6.8 %collective-permute-start.12 = (bf16[1,16,16,128]{3,1,0,2:T(8,128)(2,1)S(1)}, bf16[1,16,16,128]{3,1,0,2:T(8,128)(2,1)S(1)}, u32[]{:S(2)}, u32[]{:S(2)}) collective-permute-start(bf16[1,16,16,128]{3,1,0,2:T(8,128)(2,1)S(1)} %get-tuple-element.51), channel_id=1, source_target_pairs={{0,26},{2,28},{4,30},{6,0},{8,2},{10,4},{12,6},{14,8},{16,10},{18,... | collective-permute-start | bytes 196616 | tf_op jit(solution)/shard_map/ppermute | solution.py:39
  290.5 1.9 collective-permute-start.14
  308.7 2.9 copy.63
  311.6 5.9 %all-to-all-start.4 = ((bf16[2,16,256,128]{3,1,0,2:T(8,128)(2,1)}), bf16[2,16,256,128]{3,1,0,2:T(8,128)(2,1)}, u32[]{:S(2)}, u32[]{:S(2)}) async-start(bf16[2,16,256,128]{3,1,0,2:T(8,128)(2,1)} %copy.63), calls=%async_computation.4 | async-start | bytes 4194304 | tf_op jit(solution)/shard_map/all_to_all | solution.py:127
  317.5 3.0 fusion.52
  322.2 2.7 copy.58
  324.9 38.8 %all-to-all-done.4 = bf16[2,16,256,128]{3,1,0,2:T(8,128)(2,1)} async-done(((bf16[2,16,256,128]{3,1,0,2:T(8,128)(2,1)}), bf16[2,16,256,128]{3,1,0,2:T(8,128)(2,1)}, u32[]{:S(2)}, u32[]{:S(2)}) %all-to-all-start.4) | async-done | bytes 2097184 | tf_op jit(solution)/shard_map/all_to_all | solution.py:127
  363.7 6.1 %all-to-all-start.3 = ((bf16[2,16,256,128]{3,1,0,2:T(8,128)(2,1)}), bf16[2,16,256,128]{3,1,0,2:T(8,128)(2,1)}, u32[]{:S(2)}, u32[]{:S(2)}) async-start(bf16[2,16,256,128]{3,1,0,2:T(8,128)(2,1)} %copy.58), calls=%async_computation.3 | async-start | bytes 4194304 | tf_op jit(solution)/shard_map/all_to_all | solution.py:128
  369.8 2.4 copy.64
  372.2 1.7 slice_convert_fusion
  374.5 41.5 %all-to-all-done.3 = bf16[2,16,256,128]{3,1,0,2:T(8,128)(2,1)} async-done(((bf16[2,16,256,128]{3,1,0,2:T(8,128)(2,1)}), bf16[2,16,256,128]{3,1,0,2:T(8,128)(2,1)}, u32[]{:S(2)}, u32[]{:S(2)}) %all-to-all-start.3) | async-done | bytes 2097184 | tf_op jit(solution)/shard_map/all_to_all | solution.py:128
  416.0 2.4 copy.59
  419.9 4.6 fusion.56
  424.5 4.6 fusion.55
  431.0 1.8 multiply_convert_fusion.1
  432.8 12.0 %fusion.12 = f32[3,16,256,256]{3,2,1,0:T(8,128)} fusion(f32[256,3,16,128]{3,0,2,1:T(8,128)} %fusion.56, bf16[1,256,16,128]{3,1,2,0:T(8,128)(2,1)} %copy.71, bf16[1,256,16,128]{3,1,2,0:T(8,128)(2,1)} %get-tuple-element.19, bf16[1,256,16,128]{3,1,2,0:T(8,128)(2,1)S(1)} %get-tuple-element.18, f32[128]{0:T(128)S(1)} %fusion.177), kind=kOutput, calls=%fused_computation.31 | convolution fusion | flops 1624768512 | bytes 22020608 | tf_op jit(solution)/shard_map/...zwk,kx->...zwx/dot_general | solution.py:68
  444.8 12.1 %convolution_subtract_fusion = f32[3,16,256,256]{3,2,1,0:T(8,128)} fusion(f32[3,16,256,256]{3,2,1,0:T(8,128)} %fusion.12, f32[256,3,16,128]{3,0,2,1:T(8,128)} %fusion.55, bf16[1,256,16,128]{3,1,2,0:T(8,128)(2,1)} %copy.71, bf16[1,256,16,128]{3,1,2,0:T(8,128)(2,1)} %get-tuple-element.19, bf16[1,256,16,128]{3,1,2,0:T(8,128)(2,1)S(1)} %get-tuple-element.18, ...), kind=kOutput, calls=%fused_computation.10 | convolution fusion | flops 1627914240 | bytes 34603520 | tf_op jit(solution)/shard_map/...zwk,kx->...zwx/dot_general | solution.py:68
  456.9 7.2 %fusion.42 = bf16[16,256,256]{2,1,0:T(8,128)(2,1)S(1)} fusion(f32[3,16,256,256]{3,2,1,0:T(8,128)} %convolution_subtract_fusion, bf16[3,16,256,256]{3,2,1,0:T(8,128)(2,1)} %all-gather.2.cloned.1.call-done), kind=kLoop, calls=%fused_computation.59 | loop fusion | flops 9437184 | bytes 20971520 | tf_op jit(solution)/shard_map/add | solution.py:139
  467.8 2.7 fusion.84
  471.9 1.6 copy.72
  473.5 6.4 %all-to-all-start.5 = ((bf16[256,16,128]{2,1,0:T(8,128)(2,1)}), bf16[256,16,128]{2,1,0:T(8,128)(2,1)}, u32[]{:S(2)}, u32[]{:S(2)}) async-start(bf16[256,16,128]{2,1,0:T(8,128)(2,1)} %copy.72), calls=%async_computation.5 | async-start | bytes 2097152 | tf_op jit(solution)/shard_map/all_to_all | solution.py:153
  480.0 2.9 subtract_convert_fusion.4
  486.0 19.3 %collective-permute-start.16 = (bf16[1,16,16,128]{3,1,0,2:T(8,128)(2,1)S(1)}, bf16[1,16,16,128]{3,1,0,2:T(8,128)(2,1)S(1)}, u32[]{:S(2)}, u32[]{:S(2)}) collective-permute-start(bf16[1,16,16,128]{3,1,0,2:T(8,128)(2,1)S(1)} %get-tuple-element.47), channel_id=1, source_target_pairs={{0,4},{2,6},{4,8},{6,10},{8,12},{10,14},{12,16},{14,18},{16,20},{1... | collective-permute-start | bytes 196616 | tf_op jit(solution)/shard_map/ppermute | solution.py:39
  505.3 2.2 collective-permute-start.17
  507.6 1.9 collective-permute-start.20
  509.5 3.2 collective-permute-start.21
  512.8 2.7 collective-permute-start.22
  516.5 2.4 collective-permute-start.24
  518.9 4.6 collective-permute-start.25
  523.5 3.6 collective-permute-start.26
  527.1 2.9 collective-permute-start.27
  531.5 1.8 collective-permute-done.28
  539.3 2.1 fusion.39
  541.5 2.1 fusion.35
  543.5 2.3 maximum_bitcast_fusion
  (166 shorter events, 64.8 us)
Async XLA Ops:
  7.2 3.5 copy-start
  11.2 1.6 copy-start.11
  17.1 52.7 %all-to-all-start.1 = ((bf16[2,16,256,128]{3,1,0,2:T(8,128)(2,1)}), bf16[2,16,256,128]{3,1,0,2:T(8,128)(2,1)}, u32[]{:S(2)}, u32[]{:S(2)}) async-start(bf16[2,16,256,128]{3,1,0,2:T(8,128)(2,1)} %copy.46), calls=%async_computation.1 | async-start | bytes 4194304 | tf_op jit(solution)/shard_map/all_to_all | solution.py:127
  23.7 1.6 copy-start.12
  69.9 52.3 %all-to-all-start = ((bf16[2,16,256,128]{3,1,0,2:T(8,128)(2,1)}), bf16[2,16,256,128]{3,1,0,2:T(8,128)(2,1)S(1)}, u32[]{:S(2)}, u32[]{:S(2)}) async-start(bf16[2,16,256,128]{3,1,0,2:T(8,128)(2,1)} %copy.41), calls=%async_computation | async-start | bytes 4194304 | tf_op jit(solution)/shard_map/all_to_all | solution.py:128
  76.0 83.2 %all-gather.2.cloned.1.call-start = ((), (), s32[]{:S(2)}) async-start(), calls=%async_computation.6 | async-start | bytes 9437184 | tf_op jit(solution)/shard_map/all_gather | solution.py:106
  123.5 1.6 copy-start.14
  125.3 1.2 copy-start.15
  177.0 118.3 %all-to-all-start.2 = ((bf16[256,16,128]{2,1,0:T(8,128)(2,1)}), bf16[256,16,128]{2,1,0:T(8,128)(2,1)}, u32[]{:S(2)}, u32[]{:S(2)}) async-start(bf16[256,16,128]{2,1,0:T(8,128)(2,1)} %copy.55), calls=%async_computation.2 | async-start | bytes 2097152 | tf_op jit(solution)/shard_map/all_to_all | solution.py:153
  183.5 4.7 copy-start.1
  186.7 39.9 %collective-permute-start = (bf16[1,16,16,128]{3,1,0,2:T(8,128)(2,1)S(1)}, bf16[1,16,16,128]{3,1,0,2:T(8,128)(2,1)S(1)}, u32[]{:S(2)}, u32[]{:S(2)}) collective-permute-start(bf16[1,16,16,128]{3,1,0,2:T(8,128)(2,1)S(1)} %constant_dynamic-slice_fusion.29), channel_id=1, source_target_pairs={{0,2},{2,4},{4,6},{6,8},{8,10},{10,12},{12,14},{14,16},{16,18},{18... | collective-permute-start | bytes 196616 | tf_op jit(solution)/shard_map/ppermute | solution.py:39
  189.8 40.0 %copy-start.16 = (f32[64]{0:T(128)S(1)}, f32[64]{0:T(128)}, u32[]{:S(2)}) copy-start(f32[64]{0:T(128)} %param.8) | copy-start | bytes 772
  226.9 44.8 %collective-permute-start.1 = (bf16[1,16,16,128]{3,1,0,2:T(8,128)(2,1)S(1)}, bf16[1,16,16,128]{3,1,0,2:T(8,128)(2,1)S(1)}, u32[]{:S(2)}, u32[]{:S(2)}) collective-permute-start(bf16[1,16,16,128]{3,1,0,2:T(8,128)(2,1)S(1)} %get-tuple-element.62), channel_id=1, source_target_pairs={{0,4},{2,6},{4,8},{6,10},{8,12},{10,14},{12,16},{14,18},{16,20},{1... | collective-permute-start | bytes 196616 | tf_op jit(solution)/shard_map/ppermute | solution.py:39
  256.8 15.3 %collective-permute-start.2 = (bf16[1,16,16,128]{3,1,0,2:T(8,128)(2,1)S(1)}, bf16[1,16,16,128]{3,1,0,2:T(8,128)(2,1)S(1)}, u32[]{:S(2)}, u32[]{:S(2)}) collective-permute-start(bf16[1,16,16,128]{3,1,0,2:T(8,128)(2,1)S(1)} %get-tuple-element.61), channel_id=1, source_target_pairs={{0,6},{2,8},{4,10},{6,12},{8,14},{10,16},{12,18},{14,20},{16,22},{... | collective-permute-start | bytes 196616 | tf_op jit(solution)/shard_map/ppermute | solution.py:39
  258.8 15.9 %collective-permute-start.3 = (bf16[1,16,16,128]{3,1,0,2:T(8,128)(2,1)S(1)}, bf16[1,16,16,128]{3,1,0,2:T(8,128)(2,1)S(1)}, u32[]{:S(2)}, u32[]{:S(2)}) collective-permute-start(bf16[1,16,16,128]{3,1,0,2:T(8,128)(2,1)S(1)} %get-tuple-element.60), channel_id=1, source_target_pairs={{0,8},{2,10},{4,12},{6,14},{8,16},{10,18},{12,20},{14,22},{16,24},... | collective-permute-start | bytes 196616 | tf_op jit(solution)/shard_map/ppermute | solution.py:39
  261.9 14.9 %collective-permute-start.4 = (bf16[1,16,16,128]{3,1,0,2:T(8,128)(2,1)S(1)}, bf16[1,16,16,128]{3,1,0,2:T(8,128)(2,1)S(1)}, u32[]{:S(2)}, u32[]{:S(2)}) collective-permute-start(bf16[1,16,16,128]{3,1,0,2:T(8,128)(2,1)S(1)} %get-tuple-element.59), channel_id=1, source_target_pairs={{0,10},{2,12},{4,14},{6,16},{8,18},{10,20},{12,22},{14,24},{16,26}... | collective-permute-start | bytes 196616 | tf_op jit(solution)/shard_map/ppermute | solution.py:39
  268.8 10.0 %collective-permute-start.5 = (bf16[1,16,16,128]{3,1,0,2:T(8,128)(2,1)S(1)}, bf16[1,16,16,128]{3,1,0,2:T(8,128)(2,1)S(1)}, u32[]{:S(2)}, u32[]{:S(2)}) collective-permute-start(bf16[1,16,16,128]{3,1,0,2:T(8,128)(2,1)S(1)} %get-tuple-element.58), channel_id=1, source_target_pairs={{0,12},{2,14},{4,16},{6,18},{8,20},{10,22},{12,24},{14,26},{16,28}... | collective-permute-start | bytes 196616 | tf_op jit(solution)/shard_map/ppermute | solution.py:39
  271.7 8.4 %collective-permute-start.6 = (bf16[1,16,16,128]{3,1,0,2:T(8,128)(2,1)S(1)}, bf16[1,16,16,128]{3,1,0,2:T(8,128)(2,1)S(1)}, u32[]{:S(2)}, u32[]{:S(2)}) collective-permute-start(bf16[1,16,16,128]{3,1,0,2:T(8,128)(2,1)S(1)} %get-tuple-element.57), channel_id=1, source_target_pairs={{0,14},{2,16},{4,18},{6,20},{8,22},{10,24},{12,26},{14,28},{16,30}... | collective-permute-start | bytes 196616 | tf_op jit(solution)/shard_map/ppermute | solution.py:39
  272.0 11.5 %collective-permute-start.7 = (bf16[1,16,16,128]{3,1,0,2:T(8,128)(2,1)S(1)}, bf16[1,16,16,128]{3,1,0,2:T(8,128)(2,1)S(1)}, u32[]{:S(2)}, u32[]{:S(2)}) collective-permute-start(bf16[1,16,16,128]{3,1,0,2:T(8,128)(2,1)S(1)} %get-tuple-element.56), channel_id=1, source_target_pairs={{0,16},{2,18},{4,20},{6,22},{8,24},{10,26},{12,28},{14,30},{16,0},... | collective-permute-start | bytes 196616 | tf_op jit(solution)/shard_map/ppermute | solution.py:39
  274.6 15.7 %collective-permute-start.8 = (bf16[1,16,16,128]{3,1,0,2:T(8,128)(2,1)S(1)}, bf16[1,16,16,128]{3,1,0,2:T(8,128)(2,1)S(1)}, u32[]{:S(2)}, u32[]{:S(2)}) collective-permute-start(bf16[1,16,16,128]{3,1,0,2:T(8,128)(2,1)S(1)} %get-tuple-element.55), channel_id=1, source_target_pairs={{0,18},{2,20},{4,22},{6,24},{8,26},{10,28},{12,30},{14,0},{16,2},{... | collective-permute-start | bytes 196616 | tf_op jit(solution)/shard_map/ppermute | solution.py:39
  276.8 13.6 %collective-permute-start.9 = (bf16[1,16,16,128]{3,1,0,2:T(8,128)(2,1)S(1)}, bf16[1,16,16,128]{3,1,0,2:T(8,128)(2,1)S(1)}, u32[]{:S(2)}, u32[]{:S(2)}) collective-permute-start(bf16[1,16,16,128]{3,1,0,2:T(8,128)(2,1)S(1)} %get-tuple-element.54), channel_id=1, source_target_pairs={{0,20},{2,22},{4,24},{6,26},{8,28},{10,30},{12,0},{14,2},{16,4},{1... | collective-permute-start | bytes 196616 | tf_op jit(solution)/shard_map/ppermute | solution.py:39
  278.8 13.5 %collective-permute-start.10 = (bf16[1,16,16,128]{3,1,0,2:T(8,128)(2,1)S(1)}, bf16[1,16,16,128]{3,1,0,2:T(8,128)(2,1)S(1)}, u32[]{:S(2)}, u32[]{:S(2)}) collective-permute-start(bf16[1,16,16,128]{3,1,0,2:T(8,128)(2,1)S(1)} %get-tuple-element.53), channel_id=1, source_target_pairs={{0,22},{2,24},{4,26},{6,28},{8,30},{10,0},{12,2},{14,4},{16,6},{18... | collective-permute-start | bytes 196616 | tf_op jit(solution)/shard_map/ppermute | solution.py:39
  280.2 12.2 %collective-permute-start.11 = (bf16[1,16,16,128]{3,1,0,2:T(8,128)(2,1)S(1)}, bf16[1,16,16,128]{3,1,0,2:T(8,128)(2,1)S(1)}, u32[]{:S(2)}, u32[]{:S(2)}) collective-permute-start(bf16[1,16,16,128]{3,1,0,2:T(8,128)(2,1)S(1)} %get-tuple-element.52), channel_id=1, source_target_pairs={{0,24},{2,26},{4,28},{6,30},{8,0},{10,2},{12,4},{14,6},{16,8},{18,... | collective-permute-start | bytes 196616 | tf_op jit(solution)/shard_map/ppermute | solution.py:39
  283.5 8.9 %collective-permute-start.12 = (bf16[1,16,16,128]{3,1,0,2:T(8,128)(2,1)S(1)}, bf16[1,16,16,128]{3,1,0,2:T(8,128)(2,1)S(1)}, u32[]{:S(2)}, u32[]{:S(2)}) collective-permute-start(bf16[1,16,16,128]{3,1,0,2:T(8,128)(2,1)S(1)} %get-tuple-element.51), channel_id=1, source_target_pairs={{0,26},{2,28},{4,30},{6,0},{8,2},{10,4},{12,6},{14,8},{16,10},{18,... | collective-permute-start | bytes 196616 | tf_op jit(solution)/shard_map/ppermute | solution.py:39
  290.4 3.7 collective-permute-start.13
  290.5 4.2 collective-permute-start.14
  301.0 1.5 copy-start.4
  301.1 2.9 copy-start.2
  305.4 1.6 copy-start.6
  305.4 1.6 copy-start.7
  305.4 1.6 copy-start.9
  311.6 52.1 %all-to-all-start.4 = ((bf16[2,16,256,128]{3,1,0,2:T(8,128)(2,1)}), bf16[2,16,256,128]{3,1,0,2:T(8,128)(2,1)}, u32[]{:S(2)}, u32[]{:S(2)}) async-start(bf16[2,16,256,128]{3,1,0,2:T(8,128)(2,1)} %copy.63), calls=%async_computation.4 | async-start | bytes 4194304 | tf_op jit(solution)/shard_map/all_to_all | solution.py:127
  317.5 3.0 copy-start.8
  317.5 3.0 copy-start.10
  363.7 52.3 %all-to-all-start.3 = ((bf16[2,16,256,128]{3,1,0,2:T(8,128)(2,1)}), bf16[2,16,256,128]{3,1,0,2:T(8,128)(2,1)}, u32[]{:S(2)}, u32[]{:S(2)}) async-start(bf16[2,16,256,128]{3,1,0,2:T(8,128)(2,1)} %copy.58), calls=%async_computation.3 | async-start | bytes 4194304 | tf_op jit(solution)/shard_map/all_to_all | solution.py:128
  429.0 1.8 copy-start.13
  473.5 61.1 %all-to-all-start.5 = ((bf16[256,16,128]{2,1,0:T(8,128)(2,1)}), bf16[256,16,128]{2,1,0:T(8,128)(2,1)}, u32[]{:S(2)}, u32[]{:S(2)}) async-start(bf16[256,16,128]{2,1,0:T(8,128)(2,1)} %copy.72), calls=%async_computation.5 | async-start | bytes 2097152 | tf_op jit(solution)/shard_map/all_to_all | solution.py:153
  482.9 2.8 collective-permute-start.15
  486.0 23.5 %collective-permute-start.16 = (bf16[1,16,16,128]{3,1,0,2:T(8,128)(2,1)S(1)}, bf16[1,16,16,128]{3,1,0,2:T(8,128)(2,1)S(1)}, u32[]{:S(2)}, u32[]{:S(2)}) collective-permute-start(bf16[1,16,16,128]{3,1,0,2:T(8,128)(2,1)S(1)} %get-tuple-element.47), channel_id=1, source_target_pairs={{0,4},{2,6},{4,8},{6,10},{8,12},{10,14},{12,16},{14,18},{16,20},{1... | collective-permute-start | bytes 196616 | tf_op jit(solution)/shard_map/ppermute | solution.py:39
  505.3 7.4 %collective-permute-start.17 = (bf16[1,16,16,128]{3,1,0,2:T(8,128)(2,1)S(1)}, bf16[1,16,16,128]{3,1,0,2:T(8,128)(2,1)S(1)}, u32[]{:S(2)}, u32[]{:S(2)}) collective-permute-start(bf16[1,16,16,128]{3,1,0,2:T(8,128)(2,1)S(1)} %get-tuple-element.46), channel_id=1, source_target_pairs={{0,6},{2,8},{4,10},{6,12},{8,14},{10,16},{12,18},{14,20},{16,22},{... | collective-permute-start | bytes 196616 | tf_op jit(solution)/shard_map/ppermute | solution.py:39
  507.5 8.0 %collective-permute-start.18 = (bf16[1,16,16,128]{3,1,0,2:T(8,128)(2,1)S(1)}, bf16[1,16,16,128]{3,1,0,2:T(8,128)(2,1)S(1)}, u32[]{:S(2)}, u32[]{:S(2)}) collective-permute-start(bf16[1,16,16,128]{3,1,0,2:T(8,128)(2,1)S(1)} %get-tuple-element.45), channel_id=1, source_target_pairs={{0,8},{2,10},{4,12},{6,14},{8,16},{10,18},{12,20},{14,22},{16,24},... | collective-permute-start | bytes 196616 | tf_op jit(solution)/shard_map/ppermute | solution.py:39
  507.5 9.0 %collective-permute-start.19 = (bf16[1,16,16,128]{3,1,0,2:T(8,128)(2,1)S(1)}, bf16[1,16,16,128]{3,1,0,2:T(8,128)(2,1)S(1)}, u32[]{:S(2)}, u32[]{:S(2)}) collective-permute-start(bf16[1,16,16,128]{3,1,0,2:T(8,128)(2,1)S(1)} %get-tuple-element.44), channel_id=1, source_target_pairs={{0,10},{2,12},{4,14},{6,16},{8,18},{10,20},{12,22},{14,24},{16,26}... | collective-permute-start | bytes 196616 | tf_op jit(solution)/shard_map/ppermute | solution.py:39
  507.6 11.3 %collective-permute-start.20 = (bf16[1,16,16,128]{3,1,0,2:T(8,128)(2,1)S(1)}, bf16[1,16,16,128]{3,1,0,2:T(8,128)(2,1)S(1)}, u32[]{:S(2)}, u32[]{:S(2)}) collective-permute-start(bf16[1,16,16,128]{3,1,0,2:T(8,128)(2,1)S(1)} %get-tuple-element.43), channel_id=1, source_target_pairs={{0,12},{2,14},{4,16},{6,18},{8,20},{10,22},{12,24},{14,26},{16,28}... | collective-permute-start | bytes 196616 | tf_op jit(solution)/shard_map/ppermute | solution.py:39
  509.5 14.0 %collective-permute-start.21 = (bf16[1,16,16,128]{3,1,0,2:T(8,128)(2,1)S(1)}, bf16[1,16,16,128]{3,1,0,2:T(8,128)(2,1)S(1)}, u32[]{:S(2)}, u32[]{:S(2)}) collective-permute-start(bf16[1,16,16,128]{3,1,0,2:T(8,128)(2,1)S(1)} %get-tuple-element.42), channel_id=1, source_target_pairs={{0,14},{2,16},{4,18},{6,20},{8,22},{10,24},{12,26},{14,28},{16,30}... | collective-permute-start | bytes 196616 | tf_op jit(solution)/shard_map/ppermute | solution.py:39
  512.8 14.4 %collective-permute-start.22 = (bf16[1,16,16,128]{3,1,0,2:T(8,128)(2,1)S(1)}, bf16[1,16,16,128]{3,1,0,2:T(8,128)(2,1)S(1)}, u32[]{:S(2)}, u32[]{:S(2)}) collective-permute-start(bf16[1,16,16,128]{3,1,0,2:T(8,128)(2,1)S(1)} %get-tuple-element.41), channel_id=1, source_target_pairs={{0,16},{2,18},{4,20},{6,22},{8,24},{10,26},{12,28},{14,30},{16,0},... | collective-permute-start | bytes 196616 | tf_op jit(solution)/shard_map/ppermute | solution.py:39
  515.5 14.6 %collective-permute-start.23 = (bf16[1,16,16,128]{3,1,0,2:T(8,128)(2,1)S(1)}, bf16[1,16,16,128]{3,1,0,2:T(8,128)(2,1)S(1)}, u32[]{:S(2)}, u32[]{:S(2)}) collective-permute-start(bf16[1,16,16,128]{3,1,0,2:T(8,128)(2,1)S(1)} %get-tuple-element.40), channel_id=1, source_target_pairs={{0,18},{2,20},{4,22},{6,24},{8,26},{10,28},{12,30},{14,0},{16,2},{... | collective-permute-start | bytes 196616 | tf_op jit(solution)/shard_map/ppermute | solution.py:39
  516.5 13.7 %collective-permute-start.24 = (bf16[1,16,16,128]{3,1,0,2:T(8,128)(2,1)S(1)}, bf16[1,16,16,128]{3,1,0,2:T(8,128)(2,1)S(1)}, u32[]{:S(2)}, u32[]{:S(2)}) collective-permute-start(bf16[1,16,16,128]{3,1,0,2:T(8,128)(2,1)S(1)} %get-tuple-element.39), channel_id=1, source_target_pairs={{0,20},{2,22},{4,24},{6,26},{8,28},{10,30},{12,0},{14,2},{16,4},{1... | collective-permute-start | bytes 196616 | tf_op jit(solution)/shard_map/ppermute | solution.py:39
  518.9 12.5 %collective-permute-start.25 = (bf16[1,16,16,128]{3,1,0,2:T(8,128)(2,1)S(1)}, bf16[1,16,16,128]{3,1,0,2:T(8,128)(2,1)S(1)}, u32[]{:S(2)}, u32[]{:S(2)}) collective-permute-start(bf16[1,16,16,128]{3,1,0,2:T(8,128)(2,1)S(1)} %get-tuple-element.38), channel_id=1, source_target_pairs={{0,22},{2,24},{4,26},{6,28},{8,30},{10,0},{12,2},{14,4},{16,6},{18... | collective-permute-start | bytes 196616 | tf_op jit(solution)/shard_map/ppermute | solution.py:39
  523.5 7.9 %collective-permute-start.26 = (bf16[1,16,16,128]{3,1,0,2:T(8,128)(2,1)S(1)}, bf16[1,16,16,128]{3,1,0,2:T(8,128)(2,1)S(1)}, u32[]{:S(2)}, u32[]{:S(2)}) collective-permute-start(bf16[1,16,16,128]{3,1,0,2:T(8,128)(2,1)S(1)} %get-tuple-element.37), channel_id=1, source_target_pairs={{0,24},{2,26},{4,28},{6,30},{8,0},{10,2},{12,4},{14,6},{16,8},{18,... | collective-permute-start | bytes 196616 | tf_op jit(solution)/shard_map/ppermute | solution.py:39
  527.1 4.3 collective-permute-start.27
  530.1 3.2 collective-permute-start.28
  530.2 3.8 collective-permute-start.29
  536.2 2.7 copy-start.3
  537.5 1.8 copy-start.5
Sparse Core Ops, SparseCore 0:
  78.3 80.8 all-gather.1
